TPU v7x, 32 devices: a whole 2x2x4 slice. The times are simulated.
32 devices in a mesh: groups: 2 (over x), expert: 16 (over z, y, core).
Axes of the slice: x: 2, y: 2, z: 4, core: 2. Of those that a mesh axis runs over, the one named last changes fastest.
Arguments:
- tokens: bfloat16 [4096, 7168], P(('groups', 'expert')), parts along dimension 0, may hold values from -6 to 6
- route_ids: int32 [4096, 2], P(('groups', 'expert')), parts along dimension 0, may hold values from 0 to 3, all different within a row; in each aligned block of 128 rows (0 to 127, 128 to 255, ...) at most 80 rows name the same one
- levels: int32 [4096, 2], P(('groups', 'expert')), parts along dimension 0, may hold values from 1 to 64
- w_gate: bfloat16 [16, 7168, 512], P('expert'), may hold values from -0.0625 to 0.0625
- w_up: bfloat16 [16, 7168, 512], P('expert'), may hold values from -0.0625 to 0.0625
- w_down: bfloat16 [16, 512, 7168], P('expert'), may hold values from -0.125 to 0.125
Outputs:
- combined: bfloat16 [4096, 7168], P(('groups', 'expert')), parts along dimension 0
There are 2 independent parts, one for each index of `groups`. A program takes and returns all parts, laid end to end along the dimension named above; an argument that names none is the same for every part. Nothing has to cross between parts.
Inputs may be any that keep to these rules, and one draw needn't show every extreme that they name: `route_ids`: each row names 2 different experts; among the rows of one device no expert is named more than 80 times, a bound that some block reaches.
All inputs are finite; a program needn't handle non-finite values.
Results may differ from a plain program's by a relative error of at most 0.013.
Values may be sent and summed in bfloat16 or wider, within the bound.
A program may use at most 192 MiB of HBM per device.

v0:
```python
import jax
import jax.numpy as jnp
from jax import lax
from jax.sharding import PartitionSpec as P

SHARDS = 4


def on_device(tokens, route_ids, levels, w_gate, w_up, w_down):
    tok_rows, width = tokens.shape
    top = route_ids.shape[1]
    devices = lax.axis_size("expert")
    experts = devices // SHARDS
    capacity = 5 * tok_rows * top // (4 * experts)
    flat_ids = route_ids.reshape(-1)
    count = flat_ids.shape[0]
    onehot = (flat_ids[:, None] == jnp.arange(experts, dtype=jnp.int32)[None, :]).astype(jnp.int32)
    before = jnp.cumsum(onehot, axis=0) - onehot
    slot_pos = jnp.sum(before * onehot, axis=1)
    target = flat_ids * capacity + slot_pos
    source = jnp.arange(count, dtype=jnp.int32) // top
    owner = jnp.full((experts * capacity,), tok_rows, jnp.int32).at[target].set(source)
    padded = jnp.concatenate([tokens, jnp.zeros((1, width), tokens.dtype)], axis=0)
    outgoing = padded[owner].reshape(experts, capacity, width)
    copies = jnp.broadcast_to(outgoing[:, None], (experts, SHARDS, capacity, width)).reshape(
        devices, capacity, width
    )
    arrived = lax.all_to_all(copies, "expert", split_axis=0, concat_axis=0, tiled=True)
    inputs = arrived.reshape(devices * capacity, width)
    gate = jnp.dot(inputs, w_gate[0], preferred_element_type=jnp.float32)
    up = jnp.dot(inputs, w_up[0], preferred_element_type=jnp.float32)
    hidden = (jax.nn.silu(gate) * up).astype(jnp.bfloat16)
    partial_out = jnp.dot(hidden, w_down[0], preferred_element_type=jnp.float32).astype(
        jnp.bfloat16
    )
    partial_out = partial_out.reshape(devices, capacity, width)
    returned = lax.all_to_all(partial_out, "expert", split_axis=0, concat_axis=0, tiled=True)
    grouped = returned.reshape(experts, SHARDS, capacity, width)
    expert_out = jnp.sum(grouped.astype(jnp.float32), axis=1).astype(jnp.bfloat16)
    picked = expert_out.reshape(experts * capacity, width)[target].reshape(tok_rows, top, width)
    level_f = levels.astype(jnp.float32)
    weights = level_f / jnp.sum(level_f, axis=1, keepdims=True)
    combined = jnp.einsum("tkd,tk->td", picked.astype(jnp.float32), weights)
    return combined.astype(jnp.bfloat16)


def solution(mesh):
    return jax.shard_map(
        on_device,
        mesh=mesh,
        in_specs=(
            P(("groups", "expert"), None),
            P(("groups", "expert"), None),
            P(("groups", "expert"), None),
            P("expert", None, None),
            P("expert", None, None),
            P("expert", None, None),
        ),
        out_specs=P(("groups", "expert"), None),
        check_vma=False,
    )
```

profile of v0, /device:TPU:13, one launch (start us, length us, event | category | flops | bytes accessed | tf_op | source)
XLA Modules:
  0.0 903.4 jit_solution(16745211734803782363)
XLA Ops:
  0.0 0.8 copy.10
  0.8 0.1 eq.29
  0.9 0.1 eq.25
  1.1 0.7 broadcast_multiply_fusion
  1.8 1.2 reduce-window.6
  3.0 0.1 slice.12
  3.1 0.1 copy.12
  3.2 0.1 copy.13
  3.3 0.1 add_bitcast_fusion
  3.4 0.1 copy.9
  3.5 0.1 mul.28
  3.7 1.4 scatter_custom_fusion
  5.1 1.7 concatenate.3
  6.8 6.1 gather_fusion
  12.9 4.3 broadcast_in_dim.21
  17.2 401.9 %all_to_all.10 = bf16[16,80,7168]{2,1,0:T(8,128)(2,1)S(1)} all-to-all(bf16[16,80,7168]{2,1,0:T(8,128)(2,1)S(1)} %bitcast.52), channel_id=1, replica_groups=mesh['groups'=2,'expert'=16] {'expert'}, dimensions={0} | all-to-all | bytes 36700160 | tf_op jit(solution)/shard_map/all_to_all | solution.py:28
  419.1 13.7 %fusion.3 = f32[1280,512]{1,0:T(8,128)} fusion(bf16[1280,7168]{1,0:T(8,128)(2,1)S(1)} %bitcast.54, bf16[1,7168,512]{2,1,0:T(8,128)(2,1)} %param.9), kind=kOutput, calls=%fused_computation.8 | convolution fusion | flops 9395240960 | bytes 28311552 | tf_op jit(solution)/shard_map/dot_general | solution.py:30
  432.8 13.2 %fusion.8 = bf16[1280,512]{1,0:T(8,128)(2,1)S(1)} fusion(bf16[1280,7168]{1,0:T(8,128)(2,1)S(1)} %bitcast.55, bf16[1,7168,512]{2,1,0:T(8,128)(2,1)} %param.10, f32[1280,512]{1,0:T(8,128)} %fusion.3), kind=kOutput, calls=%fused_computation.12 | convolution fusion | flops 9399173120 | bytes 29622272 | tf_op jit(solution)/shard_map/dot_general | solution.py:31
  446.1 15.8 %convolution_convert_fusion = bf16[1280,7168]{1,0:T(8,128)(2,1)} fusion(bf16[1280,512]{1,0:T(8,128)(2,1)S(1)} %fusion.8, bf16[1,512,7168]{2,1,0:T(8,128)(2,1)} %param.11), kind=kOutput, calls=%fused_computation.3 | convolution fusion | flops 9404416000 | bytes 27000832 | tf_op jit(solution)/shard_map/dot_general | solution.py:33
  461.8 0.0 copy-start
  461.8 6.7 all-to-all-start.1
  468.5 0.0 copy-done
  468.6 0.1 copy.14
  468.7 395.6 %all-to-all-done.1 = bf16[16,80,7168]{2,1,0:T(8,128)(2,1)} async-done(((bf16[16,80,7168]{2,1,0:T(8,128)(2,1)}), bf16[16,80,7168]{2,1,0:T(8,128)(2,1)}, u32[]{:S(2)}, u32[]{:S(2)}) %all-to-all-start.1) | async-done | bytes 18350112 | tf_op jit(solution)/shard_map/all_to_all | solution.py:37
  864.4 12.6 %bitcast_reduce_fusion = bf16[4,80,7168]{2,1,0:T(8,128)(2,1)} fusion(bf16[16,80,7168]{2,1,0:T(8,128)(2,1)} %all-to-all-done.1), kind=kLoop, calls=%fused_computation.4 | loop fusion | flops 6881280 | bytes 22937600 | tf_op jit(solution)/shard_map/reduce_sum | solution.py:39
  876.9 10.9 %gather_fusion.1 = bf16[256,7168]{1,0:T(8,128)(2,1)} fusion(bf16[320,7168]{1,0:T(8,128)(2,1)} %bitcast.51, s32[1024]{0:T(1024)S(1)} %pad_clamp_fusion), kind=kCustom, calls=%fused_computation.1 | custom fusion | bytes 7341056 | tf_op jit(solution)/shard_map/gather | solution.py:40
  887.8 8.1 reshape.72
  895.9 5.6 fusion.16
  901.6 1.8 copy.19
  (11 shorter events, 0.1 us)
Async XLA Ops:
  461.8 6.7 copy-start
  461.8 402.5 %all-to-all-start.1 = ((bf16[16,80,7168]{2,1,0:T(8,128)(2,1)}), bf16[16,80,7168]{2,1,0:T(8,128)(2,1)}, u32[]{:S(2)}, u32[]{:S(2)}) async-start(bf16[16,80,7168]{2,1,0:T(8,128)(2,1)} %bitcast.53), calls=%async_computation.1 | async-start | bytes 36700160 | tf_op jit(solution)/shard_map/all_to_all | solution.py:37
where the time goes:
time: 904 us; the launch traced here: 903 us
  blocking collectives  402 us (44%)
  waiting for transfers between devices  396 us (44%)
  matrix products  48.3 us (5%)
  local copies, waits for them, and re-layouts  36.1 us (4%)
  other arithmetic  14.7 us (2%)
    all_to_all x1, blocking collectives, on_device(): lax.all_to_all(copies, 'expert', split_axis=0, concat_axis=0, tiled=True)  402 us
    all_to_all x1, waiting for transfers between devices, on_device(): lax.all_to_all(partial_out, 'expert', split_axis=0, concat_axis=0, tiled=...  396 us
  transfers between devices with their start and end apart: 1, of which 1 were waited for; matrix products, arithmetic and copies ran while one was open for 0% of the time, Pallas kernels for 0%

commit v1 on v0

v1 whole, which is shorter than its diff:
```python
import functools

import jax
import jax.numpy as jnp
from jax import lax
from jax.experimental import pallas as pl
from jax.experimental.pallas import tpu as pltpu
from jax.sharding import PartitionSpec as P

SHARDS = 4
MESH = pl.DeviceIdType.MESH


def tile_of(length, most):
    size = most
    while length % size:
        size //= 2
    return size


def layer_kernel(
    planes, out_ref, gate_hbm, up_hbm, down_hbm, ret_ref,
    x, gate, up, down, acc, hidden, pair, cross,
    w_sem, z_send, z_recv, y_send, y_recv, p_send, p_recv,
    rp_send, rp_recv, ry_send, ry_recv, rz_send, rz_recv,
):
    me = lax.axis_index("expert")
    plane, s = me // SHARDS, me % SHARDS
    base = plane * SHARDS
    core, row = s % 2, s // 2
    partner_s = row * 2 + (1 - core)
    cross_s = (1 - row) * 2 + core
    diag_s = (1 - row) * 2 + (1 - core)
    partner, neighbour = base + partner_s, base + cross_s
    cap, width = x.shape[2], x.shape[3]
    ff = gate.shape[1]
    rows = SHARDS * cap

    barrier = pltpu.get_barrier_semaphore()
    peers = [partner, neighbour]
    peers += [((plane + j) % planes) * SHARDS + s for j in range(1, planes)]
    for peer in peers:
        pl.semaphore_signal(barrier, inc=1, device_id={"expert": peer}, device_id_type=MESH)
    pl.semaphore_wait(barrier, planes + 1)

    def remote(src, dst, send, recv, device):
        return pltpu.make_async_remote_copy(
            src_ref=src, dst_ref=dst, send_sem=send, recv_sem=recv,
            device_id={"expert": device}, device_id_type=MESH,
        )

    def out_copy(j):
        to = (plane + j) % planes
        return remote(out_ref.at[to], x.at[j, s], z_send.at[j], z_recv.at[j], to * SHARDS + s)

    def own_copy():
        return pltpu.make_async_copy(out_ref.at[plane], x.at[0, s], z_recv.at[0])

    def y_copy(j):
        return remote(x.at[j, s], x.at[j, s], y_send.at[j], y_recv.at[j], neighbour)

    def y_arrival(j):
        return remote(x.at[j, cross_s], x.at[j, cross_s], y_send.at[j], y_recv.at[j], neighbour)

    def p_copy(j, k, slot):
        return remote(x.at[j, slot], x.at[j, slot], p_send.at[j, k], p_recv.at[j, k], partner)

    def rp_copy(j, k, slot):
        return remote(x.at[j, slot], pair.at[j, k], rp_send.at[j, k], rp_recv.at[j, k], partner)

    def ry_copy(j):
        return remote(x.at[j, cross_s], cross.at[j], ry_send.at[j], ry_recv.at[j], neighbour)

    def rz_copy(j):
        to = (plane - j + planes) % planes
        return remote(x.at[j, s], ret_ref.at[plane], rz_send.at[j], rz_recv.at[j], to * SHARDS + s)

    own_copy().start()
    for j in range(1, planes):
        out_copy(j).start()
    loads = [
        pltpu.make_async_copy(gate_hbm.at[0], gate, w_sem.at[0]),
        pltpu.make_async_copy(up_hbm.at[0], up, w_sem.at[1]),
        pltpu.make_async_copy(down_hbm.at[0], down, w_sem.at[2]),
    ]
    for load in loads:
        load.start()

    def pass_on(j):
        y_copy(j).start()
        p_copy(j, 0, s).start()

    def finish(j):
        ry_copy(j).wait_recv()
        tile = tile_of(width, 1024)

        @pl.loop(0, width // tile)
        def _(n):
            cols = pl.ds(pl.multiple_of(n * tile, tile), tile)
            total = x[j, s, :, cols].astype(jnp.float32) + pair[j, row, :, cols].astype(jnp.float32)
            x[j, s, :, cols] = (total + cross[j, :, cols].astype(jnp.float32)).astype(x.dtype)

        @pl.when(j > 0)
        def _():
            rz_copy(j).start()

        @pl.when(j == 0)
        def _():
            pltpu.make_async_copy(x.at[0, s], ret_ref.at[plane], rz_send.at[0]).start()

    own_copy().wait()
    pass_on(0)

    @pl.loop(0, planes)
    def _(j):
        @pl.when(j + 1 < planes)
        def _():
            out_copy(j + 1).wait_recv()
            pass_on(j + 1)

        y_arrival(j).wait_recv()
        p_copy(j, 1, cross_s).start()
        p_copy(j, 0, partner_s).wait_recv()
        p_copy(j, 1, diag_s).wait_recv()

        @pl.when(j == 0)
        def _():
            for load in loads:
                load.wait()

        acc[...] = jnp.zeros_like(acc)
        k_tile = tile_of(width, 1024)

        @pl.loop(0, width // k_tile)
        def _(k):
            cols = pl.ds(pl.multiple_of(k * k_tile, k_tile), k_tile)
            part = x[j, :, :, cols].reshape(rows, k_tile)
            acc[0] += jnp.dot(part, gate[cols, :], preferred_element_type=jnp.float32)
            acc[1] += jnp.dot(part, up[cols, :], preferred_element_type=jnp.float32)

        value = acc[0]
        hidden[...] = (value / (1.0 + jnp.exp(-value)) * acc[1]).astype(hidden.dtype)

        y_copy(j).wait_send()
        p_copy(j, 0, s).wait_send()
        p_copy(j, 1, cross_s).wait_send()
        n_tile = tile_of(width, 512)

        @pl.loop(0, width // n_tile)
        def _(n):
            cols = pl.ds(pl.multiple_of(n * n_tile, n_tile), n_tile)
            part = jnp.dot(hidden[...], down[:, cols], preferred_element_type=jnp.float32)
            x[j, :, :, cols] = part.astype(x.dtype).reshape(SHARDS, cap, n_tile)

        rp_copy(j, 1 - row, diag_s).start()
        rp_copy(j, row, partner_s).start()
        rp_copy(j, 1 - row, diag_s).wait_recv()
        rp_copy(j, row, partner_s).wait_recv()
        tile = tile_of(width, 1024)

        @pl.loop(0, width // tile)
        def _(n):
            cols = pl.ds(pl.multiple_of(n * tile, tile), tile)
            total = x[j, cross_s, :, cols].astype(jnp.float32) + pair[j, 1 - row, :, cols].astype(jnp.float32)
            x[j, cross_s, :, cols] = total.astype(x.dtype)

        ry_copy(j).start()

        @pl.when(j > 0)
        def _():
            finish(j - 1)

    finish(planes - 1)
    for j in range(planes):
        rp_copy(j, 1 - row, diag_s).wait_send()
        rp_copy(j, row, partner_s).wait_send()
        ry_copy(j).wait_send()
    pltpu.make_async_copy(x.at[0, s], ret_ref.at[plane], rz_send.at[0]).wait()
    for j in range(1, planes):
        out_copy(j).wait_send()
        rz_copy(j).wait()


def combine_kernel(weight_ref, ret_ref, out_ref):
    weight = weight_ref[...]
    high = weight.astype(jnp.bfloat16)
    low = (weight - high.astype(jnp.float32)).astype(jnp.bfloat16)
    total = jnp.dot(high, ret_ref[...], preferred_element_type=jnp.float32)
    total += jnp.dot(low, ret_ref[...], preferred_element_type=jnp.float32)
    out_ref[...] = total.astype(out_ref.dtype)


def on_device(tokens, route_ids, levels, w_gate, w_up, w_down):
    tok_rows, width = tokens.shape
    top = route_ids.shape[1]
    ff = w_gate.shape[2]
    experts = lax.axis_size("expert") // SHARDS
    capacity = 5 * tok_rows * top // (4 * experts)
    cap = -(-capacity // 16) * 16
    slots = experts * cap
    dtype = tokens.dtype

    chosen = route_ids[:, :, None] == jnp.arange(experts, dtype=jnp.int32)
    named = jnp.any(chosen, axis=1)
    index = jnp.arange(tok_rows, dtype=jnp.int32)
    earlier = (index[:, None] > index[None, :]).astype(jnp.bfloat16)
    rank = jnp.dot(earlier, named.astype(jnp.bfloat16), preferred_element_type=jnp.float32)
    place = jnp.where(named, rank.astype(jnp.int32), cap)
    level_f = levels.astype(jnp.float32)
    weights = level_f / jnp.sum(level_f, axis=1, keepdims=True)
    weight_e = jnp.sum(jnp.where(chosen, weights[:, :, None], 0.0), axis=1)
    spot = jnp.arange(cap, dtype=jnp.int32)
    pick = (place[:, :, None] == spot).reshape(tok_rows, slots)
    weight_m = jnp.where(pick, jnp.repeat(weight_e, cap, axis=1), 0.0)
    outgoing = lax.dot_general(
        pick.astype(dtype), tokens, (((0,), (0,)), ((), ())), preferred_element_type=jnp.float32
    ).astype(dtype).reshape(experts, cap, width)

    dma, anywhere = pltpu.SemaphoreType.DMA, pl.BlockSpec(memory_space=pl.ANY)
    rows = SHARDS * cap
    returned = pl.pallas_call(
        functools.partial(layer_kernel, experts),
        out_shape=jax.ShapeDtypeStruct((experts, cap, width), dtype),
        in_specs=[anywhere] * 4,
        out_specs=anywhere,
        scratch_shapes=[
            pltpu.VMEM((experts, SHARDS, cap, width), dtype),
            pltpu.VMEM((width, ff), dtype),
            pltpu.VMEM((width, ff), dtype),
            pltpu.VMEM((ff, width), dtype),
            pltpu.VMEM((2, rows, ff), jnp.float32),
            pltpu.VMEM((rows, ff), dtype),
            pltpu.VMEM((experts, 2, cap, width), dtype),
            pltpu.VMEM((experts, cap, width), dtype),
            dma((3,)),
            dma((experts,)), dma((experts,)),
            dma((experts,)), dma((experts,)),
            dma((experts, 2)), dma((experts, 2)),
            dma((experts, 2)), dma((experts, 2)),
            dma((experts,)), dma((experts,)),
            dma((experts,)), dma((experts,)),
        ],
        compiler_params=pltpu.CompilerParams(
            collective_id=0, has_side_effects=True, vmem_limit_bytes=67_000_000
        ),
    )(outgoing, w_gate, w_up, w_down)

    tile = tile_of(width, 1024)
    return pl.pallas_call(
        combine_kernel,
        out_shape=jax.ShapeDtypeStruct((tok_rows, width), dtype),
        grid=(width // tile,),
        in_specs=[
            pl.BlockSpec((tok_rows, slots), lambda n: (0, 0)),
            pl.BlockSpec((slots, tile), lambda n: (0, n)),
        ],
        out_specs=pl.BlockSpec((tok_rows, tile), lambda n: (0, n)),
    )(weight_m, returned.reshape(slots, width))


def solution(mesh):
    return jax.shard_map(
        on_device,
        mesh=mesh,
        in_specs=(
            P(("groups", "expert"), None),
            P(("groups", "expert"), None),
            P(("groups", "expert"), None),
            P("expert", None, None),
            P("expert", None, None),
            P("expert", None, None),
        ),
        out_specs=P(("groups", "expert"), None),
        check_vma=False,
    )
```

time: 904 us -> 297 us (0.33)
  the two profiles are of different devices: /device:TPU:13 before, /device:TPU:0 now
where the time goes in v1:
time: 297 us
  Pallas kernels  288 us (97%)
  matrix products  5.18 us (2%)
  other arithmetic  3.5 us (1%)
    pallas_call x1, Pallas kernels, on_device(): pl.pallas_call(functools.partial(layer_kernel, experts), out_shape=jax.Sh...  281 us
    pallas_call x1, Pallas kernels, on_device(): pl.pallas_call(combine_kernel, out_shape=jax.ShapeDtypeStruct((tok_rows,...  7.28 us

profile of v1, /device:TPU:0, one launch (start us, length us, event | category | flops | bytes accessed | tf_op | source)
XLA Modules:
  0.0 297.1 jit_solution(3501895000802917342)
XLA Ops:
  0.0 0.7 fusion.1
  0.7 0.7 convert_reduce_fusion
  1.4 0.7 convert_divide_fusion
  2.1 0.7 select_reduce_fusion
  2.8 0.1 fusion
  2.9 0.1 eq.39
  3.0 0.1 copy.14
  3.2 0.1 copy.15
  3.3 0.7 broadcast_select_fusion
  4.0 5.0 %convolution_convert_fusion = bf16[320,7168]{1,0:T(8,128)(2,1)} fusion(pred[128,320]{1,0:T(32,128)(4,1)S(1)} %get-tuple-element.6, bf16[128,7168]{1,0:T(8,128)(2,1)} %param.6), kind=kOutput, calls=%fused_computation | convolution fusion | flops 589496320 | bytes 6463488 | tf_op jit(solution)/shard_map/dot_general | solution.py:215
  9.1 280.7 %shard_map.64 = bf16[4,80,7168]{2,1,0:T(8,128)(2,1)} custom-call(bf16[4,80,7168]{2,1,0:T(8,128)(2,1)} %bitcast.7, bf16[1,7168,512]{2,1,0:T(8,128)(2,1)} %gate_hbm.1, bf16[1,7168,512]{2,1,0:T(8,128)(2,1)} %up_hbm.1, bf16[1,512,7168]{2,1,0:T(8,128)(2,1)} %down_hbm.1), custom_call_target="tpu_custom_call" | custom-call | tf_op jit(solution)/shard_map/pallas_call | solution.py:221
  289.8 7.3 %shard_map.65 = bf16[128,7168]{1,0:T(8,128)(2,1)} custom-call(f32[128,320]{1,0:T(8,128)} %get-tuple-element.5.weight_ref, bf16[320,7168]{1,0:T(8,128)(2,1)} %bitcast.8), custom_call_target="tpu_custom_call" | custom-call | tf_op jit(solution)/shard_map/pallas_call | solution.py:249
  (3 shorter events, 0.0 us)

commit v2 on v1

--- a/solution.py
+++ b/solution.py
@@ -16,6 +16,14 @@
     while length % size:
         size //= 2
     return size
+
+
+def xor(a, mask, count):
+    total, bit = 0, 1
+    while bit < count:
+        total += (a // bit + mask // bit) % 2 * bit
+        bit *= 2
+    return total
 
 
 def layer_kernel(
@@ -33,12 +41,13 @@
     diag_s = (1 - row) * 2 + (1 - core)
     partner, neighbour = base + partner_s, base + cross_s
     cap, width = x.shape[2], x.shape[3]
-    ff = gate.shape[1]
     rows = SHARDS * cap
+    tile = tile_of(width, 1024)
+    chunks = width // tile
 
     barrier = pltpu.get_barrier_semaphore()
     peers = [partner, neighbour]
-    peers += [((plane + j) % planes) * SHARDS + s for j in range(1, planes)]
+    peers += [xor(plane, j, planes) * SHARDS + s for j in range(1, planes)]
     for peer in peers:
         pl.semaphore_signal(barrier, inc=1, device_id={"expert": peer}, device_id_type=MESH)
     pl.semaphore_wait(barrier, planes + 1)
@@ -49,8 +58,11 @@
             device_id={"expert": device}, device_id_type=MESH,
         )
 
+    def columns(q):
+        return pl.ds(pl.multiple_of(q * tile, tile), tile)
+
     def out_copy(j):
-        to = (plane + j) % planes
+        to = xor(plane, j, planes)
         return remote(out_ref.at[to], x.at[j, s], z_send.at[j], z_recv.at[j], to * SHARDS + s)
 
     def own_copy():
@@ -65,19 +77,40 @@
     def p_copy(j, k, slot):
         return remote(x.at[j, slot], x.at[j, slot], p_send.at[j, k], p_recv.at[j, k], partner)
 
-    def rp_copy(j, k, slot):
-        return remote(x.at[j, slot], pair.at[j, k], rp_send.at[j, k], rp_recv.at[j, k], partner)
-
-    def ry_copy(j):
-        return remote(x.at[j, cross_s], cross.at[j], ry_send.at[j], ry_recv.at[j], neighbour)
-
-    def rz_copy(j):
-        to = (plane - j + planes) % planes
-        return remote(x.at[j, s], ret_ref.at[plane], rz_send.at[j], rz_recv.at[j], to * SHARDS + s)
+    def rp_copy(j, q, k, slot):
+        cols = columns(q)
+        return remote(
+            x.at[j, slot, :, cols], pair.at[j, k, :, cols],
+            rp_send.at[j, q, k], rp_recv.at[j, q, k], partner,
+        )
+
+    def ry_copy(j, q):
+        cols = columns(q)
+        return remote(
+            x.at[j, cross_s, :, cols], cross.at[j, :, cols],
+            ry_send.at[j, q], ry_recv.at[j, q], neighbour,
+        )
+
+    def rz_copy(j, q):
+        cols, to = columns(q), xor(plane, j, planes)
+        return remote(
+            x.at[j, s, :, cols], ret_ref.at[plane, :, cols],
+            rz_send.at[j, q], rz_recv.at[j, q], to * SHARDS + s,
+        )
+
+    def keep_copy(q):
+        cols = columns(q)
+        return pltpu.make_async_copy(x.at[0, s, :, cols], ret_ref.at[plane, :, cols], rz_send.at[0, q])
 
     own_copy().start()
-    for j in range(1, planes):
-        out_copy(j).start()
+    for distance in range(1, planes):
+        for to in (plane + distance, plane - distance):
+            @pl.when((to >= 0) & (to < planes))
+            def _():
+                mask = xor(plane, to, planes)
+                remote(
+                    out_ref.at[to], x.at[mask, s], z_send.at[mask], z_recv.at[mask], to * SHARDS + s
+                ).start()
     loads = [
         pltpu.make_async_copy(gate_hbm.at[0], gate, w_sem.at[0]),
         pltpu.make_async_copy(up_hbm.at[0], up, w_sem.at[1]),
@@ -86,99 +119,103 @@
     for load in loads:
         load.start()
 
-    def pass_on(j):
+    def arrive(j):
+        if j == 0:
+            own_copy().wait()
+        else:
+            out_copy(j).wait_recv()
         y_copy(j).start()
         p_copy(j, 0, s).start()
 
-    def finish(j):
-        ry_copy(j).wait_recv()
-        tile = tile_of(width, 1024)
-
-        @pl.loop(0, width // tile)
-        def _(n):
-            cols = pl.ds(pl.multiple_of(n * tile, tile), tile)
-            total = x[j, s, :, cols].astype(jnp.float32) + pair[j, row, :, cols].astype(jnp.float32)
-            x[j, s, :, cols] = (total + cross[j, :, cols].astype(jnp.float32)).astype(x.dtype)
-
-        @pl.when(j > 0)
-        def _():
-            rz_copy(j).start()
-
-        @pl.when(j == 0)
-        def _():
-            pltpu.make_async_copy(x.at[0, s], ret_ref.at[plane], rz_send.at[0]).start()
-
-    own_copy().wait()
-    pass_on(0)
-
-    @pl.loop(0, planes)
-    def _(j):
-        @pl.when(j + 1 < planes)
-        def _():
-            out_copy(j + 1).wait_recv()
-            pass_on(j + 1)
-
+    def gather(j):
         y_arrival(j).wait_recv()
         p_copy(j, 1, cross_s).start()
         p_copy(j, 0, partner_s).wait_recv()
         p_copy(j, 1, diag_s).wait_recv()
 
-        @pl.when(j == 0)
-        def _():
-            for load in loads:
-                load.wait()
-
-        acc[...] = jnp.zeros_like(acc)
-        k_tile = tile_of(width, 1024)
-
-        @pl.loop(0, width // k_tile)
-        def _(k):
-            cols = pl.ds(pl.multiple_of(k * k_tile, k_tile), k_tile)
-            part = x[j, :, :, cols].reshape(rows, k_tile)
+    def expand(j):
+        @pl.loop(0, chunks)
+        def _(q):
+            cols = columns(q)
+            part = x[j, :, :, cols].reshape(rows, tile)
+
+            @pl.when(q == 0)
+            def _():
+                acc[...] = jnp.zeros_like(acc)
+
             acc[0] += jnp.dot(part, gate[cols, :], preferred_element_type=jnp.float32)
             acc[1] += jnp.dot(part, up[cols, :], preferred_element_type=jnp.float32)
 
         value = acc[0]
         hidden[...] = (value / (1.0 + jnp.exp(-value)) * acc[1]).astype(hidden.dtype)
 
+    def contract(j):
         y_copy(j).wait_send()
         p_copy(j, 0, s).wait_send()
         p_copy(j, 1, cross_s).wait_send()
-        n_tile = tile_of(width, 512)
-
-        @pl.loop(0, width // n_tile)
-        def _(n):
-            cols = pl.ds(pl.multiple_of(n * n_tile, n_tile), n_tile)
-            part = jnp.dot(hidden[...], down[:, cols], preferred_element_type=jnp.float32)
-            x[j, :, :, cols] = part.astype(x.dtype).reshape(SHARDS, cap, n_tile)
-
-        rp_copy(j, 1 - row, diag_s).start()
-        rp_copy(j, row, partner_s).start()
-        rp_copy(j, 1 - row, diag_s).wait_recv()
-        rp_copy(j, row, partner_s).wait_recv()
-        tile = tile_of(width, 1024)
-
-        @pl.loop(0, width // tile)
-        def _(n):
-            cols = pl.ds(pl.multiple_of(n * tile, tile), tile)
-            total = x[j, cross_s, :, cols].astype(jnp.float32) + pair[j, 1 - row, :, cols].astype(jnp.float32)
-            x[j, cross_s, :, cols] = total.astype(x.dtype)
-
-        ry_copy(j).start()
-
-        @pl.when(j > 0)
-        def _():
-            finish(j - 1)
-
-    finish(planes - 1)
+
+        @pl.loop(0, chunks + 1)
+        def _(q):
+            @pl.when(q < chunks)
+            def _():
+                cols = columns(q)
+                part = jnp.dot(hidden[...], down[:, cols], preferred_element_type=jnp.float32)
+                x[j, :, :, cols] = part.astype(x.dtype).reshape(SHARDS, cap, tile)
+                rp_copy(j, q, 1 - row, diag_s).start()
+                rp_copy(j, q, row, partner_s).start()
+
+            @pl.when(q > 0)
+            def _():
+                cols = columns(q - 1)
+                rp_copy(j, q - 1, 1 - row, diag_s).wait_recv()
+                total = x[j, cross_s, :, cols].astype(jnp.float32)
+                total += pair[j, 1 - row, :, cols].astype(jnp.float32)
+                x[j, cross_s, :, cols] = total.astype(x.dtype)
+                ry_copy(j, q - 1).start()
+
+    def finish(j):
+        @pl.loop(0, chunks)
+        def _(q):
+            cols = columns(q)
+            rp_copy(j, q, row, partner_s).wait_recv()
+            total = x[j, s, :, cols].astype(jnp.float32) + pair[j, row, :, cols].astype(jnp.float32)
+            ry_copy(j, q).wait_recv()
+            x[j, s, :, cols] = (total + cross[j, :, cols].astype(jnp.float32)).astype(x.dtype)
+            if j > 0:
+                rz_copy(j, q).start()
+            else:
+                keep_copy(q).start()
+
+    order = [0, *range(2, planes), 1]
+    arrive(0)
+    arrive(1)
+    for i, j in enumerate(order):
+        gather(j)
+        if 0 < i < planes - 2:
+            arrive(order[i + 1])
+        if i == 0:
+            for load in loads:
+                load.wait()
+        expand(j)
+        contract(j)
+        if i == 0:
+            arrive(order[1])
+        else:
+            finish(order[i - 1])
+    finish(order[-1])
+
     for j in range(planes):
-        rp_copy(j, 1 - row, diag_s).wait_send()
-        rp_copy(j, row, partner_s).wait_send()
-        ry_copy(j).wait_send()
-    pltpu.make_async_copy(x.at[0, s], ret_ref.at[plane], rz_send.at[0]).wait()
-    for j in range(1, planes):
-        out_copy(j).wait_send()
-        rz_copy(j).wait()
+        @pl.loop(0, chunks)
+        def _(q):
+            rp_copy(j, q, 1 - row, diag_s).wait_send()
+            rp_copy(j, q, row, partner_s).wait_send()
+            ry_copy(j, q).wait_send()
+            if j > 0:
+                rz_copy(j, q).wait()
+            else:
+                keep_copy(q).wait()
+        if j > 0:
+            out_copy(j).wait_send()
 
 
 def combine_kernel(weight_ref, ret_ref, out_ref):
@@ -217,7 +254,7 @@
     ).astype(dtype).reshape(experts, cap, width)
 
     dma, anywhere = pltpu.SemaphoreType.DMA, pl.BlockSpec(memory_space=pl.ANY)
-    rows = SHARDS * cap
+    rows, chunks = SHARDS * cap, width // tile_of(width, 1024)
     returned = pl.pallas_call(
         functools.partial(layer_kernel, experts),
         out_shape=jax.ShapeDtypeStruct((experts, cap, width), dtype),
@@ -236,9 +273,9 @@
             dma((experts,)), dma((experts,)),
             dma((experts,)), dma((experts,)),
             dma((experts, 2)), dma((experts, 2)),
-            dma((experts, 2)), dma((experts, 2)),
-            dma((experts,)), dma((experts,)),
-            dma((experts,)), dma((experts,)),
+            dma((experts, chunks, 2)), dma((experts, chunks, 2)),
+            dma((experts, chunks)), dma((experts, chunks)),
+            dma((experts, chunks)), dma((experts, chunks)),
         ],
         compiler_params=pltpu.CompilerParams(
             collective_id=0, has_side_effects=True, vmem_limit_bytes=67_000_000

time: 297 us -> 268 us (0.902)
  Pallas kernels: 288 us -> 259 us
    pallas_call x1, Pallas kernels: 281 us -> 251 us  [on_device(): pl.pallas_call(functools.partial(layer_kernel, experts), out_shape=jax.Sh...]
where the time goes in v2:
time: 268 us
  Pallas kernels  259 us (97%)
  matrix products  5.18 us (2%)
  other arithmetic  3.5 us (1%)
    pallas_call x1, Pallas kernels, on_device(): pl.pallas_call(functools.partial(layer_kernel, experts), out_shape=jax.Sh...  251 us
    pallas_call x1, Pallas kernels, on_device(): pl.pallas_call(combine_kernel, out_shape=jax.ShapeDtypeStruct((tok_rows,...  7.29 us

profile of v2, /device:TPU:0, one launch (start us, length us, event | category | flops | bytes accessed | tf_op | source)
XLA Modules:
  0.0 267.8 jit_solution(6302047924982540394)
XLA Ops:
  0.0 0.7 fusion.1
  0.7 0.7 convert_reduce_fusion
  1.4 0.7 convert_divide_fusion
  2.1 0.7 select_reduce_fusion
  2.8 0.1 fusion
  2.9 0.1 eq.39
  3.0 0.1 copy.14
  3.2 0.1 copy.15
  3.3 0.7 broadcast_select_fusion
  4.0 5.0 %convolution_convert_fusion = bf16[320,7168]{1,0:T(8,128)(2,1)} fusion(pred[128,320]{1,0:T(32,128)(4,1)S(1)} %get-tuple-element.6, bf16[128,7168]{1,0:T(8,128)(2,1)} %param.6), kind=kOutput, calls=%fused_computation | convolution fusion | flops 589496320 | bytes 6463488 | tf_op jit(solution)/shard_map/dot_general | solution.py:252
  9.1 251.4 %shard_map.64 = bf16[4,80,7168]{2,1,0:T(8,128)(2,1)} custom-call(bf16[4,80,7168]{2,1,0:T(8,128)(2,1)} %bitcast.7, bf16[1,7168,512]{2,1,0:T(8,128)(2,1)} %gate_hbm.1, bf16[1,7168,512]{2,1,0:T(8,128)(2,1)} %up_hbm.1, bf16[1,512,7168]{2,1,0:T(8,128)(2,1)} %down_hbm.1), custom_call_target="tpu_custom_call" | custom-call | tf_op jit(solution)/shard_map/pallas_call | solution.py:258
  260.5 7.3 %shard_map.65 = bf16[128,7168]{1,0:T(8,128)(2,1)} custom-call(f32[128,320]{1,0:T(8,128)} %get-tuple-element.5.weight_ref, bf16[320,7168]{1,0:T(8,128)(2,1)} %bitcast.8), custom_call_target="tpu_custom_call" | custom-call | tf_op jit(solution)/shard_map/pallas_call | solution.py:286
  (3 shorter events, 0.0 us)
